TPU v7x, 32 devices: a whole 2x2x4 slice. The times are simulated.
32 devices in a mesh: gx: 4 (over z), gy: 2 (over x), gz: 4 (over y, core).
Axes of the slice: x: 2, y: 2, z: 4, core: 2. Of those that a mesh axis runs over, the one named last changes fastest.
Arguments:
- start_potential: float32 [64, 256, 512], P('gx', 'gy', 'gz'), may hold values from -0.9 to 2.1
- permittivity: float32 [64, 256, 512], P('gx', 'gy', 'gz'), may hold values from 1 to 8
- screening: float32 [64, 256, 512], P('gx', 'gy', 'gz'), may hold values from 0.05 to 2
- source: float32 [64, 256, 512], P('gx', 'gy', 'gz'), may hold values from -12 to 12
Outputs:
- potential: float32 [64, 256, 512], P('gx', 'gy', 'gz')
- residual_rms: float32 [3], replicated
- induced_charge: float32 [3], replicated
All inputs are finite; a program needn't handle non-finite values.
Results may differ from a plain program's by a relative error of at most 0.0003.
Values sent between devices are 32-bit elements; how exact they have to be, the bound alone decides.
No kernel may reach another device: no remote copies, remote signals or barrier semaphores. Data moves between devices by JAX's collectives and lax.ppermute only.
A program may use at most 64 MiB of HBM per device.

v0:
```python
import jax
import jax.numpy as jnp
from jax import lax
from jax.sharding import PartitionSpec as P

ITERS = 3


def padded_2(array, sides, width):
    for axis, dim in sides:
        size, length = (lax.axis_size(axis), array.shape[dim])
        up = [(i, (i + 1) % size) for i in range(size - 1)]
        down = [(j, i) for i, j in up]
        last = lax.slice_in_dim(array, length - width, length, axis=dim)
        initial = lax.slice_in_dim(array, 0, width, axis=dim)
        before = lax.ppermute(last, axis, up)
        after = lax.ppermute(initial, axis, down)
        array = jnp.concatenate([before, array, after], axis=dim)
    return array


def harmonic(left, right):
    total = left + right
    return 2.0 * left * right / jnp.where(total > 0, total, 1.0)


def neighbours(block):
    return [
        block[2:, 1:-1, 1:-1],
        block[:-2, 1:-1, 1:-1],
        block[1:-1, 2:, 1:-1],
        block[1:-1, :-2, 1:-1],
        block[1:-1, 1:-1, 2:],
        block[1:-1, 1:-1, :-2],
    ]


def relax(padded, weights_pad, screening, source):
    center = padded[1:-1, 1:-1, 1:-1]
    middle = weights_pad[1:-1, 1:-1, 1:-1]
    flux = jnp.zeros_like(center)
    diagonal = jnp.zeros_like(center)
    for near, other in zip(neighbours(padded), neighbours(weights_pad)):
        weight = harmonic(middle, other)
        flux = flux + weight * (center - near)
        diagonal = diagonal + weight
    induced = screening * jnp.sinh(center)
    residual = source - flux - induced
    diagonal = diagonal + screening * jnp.cosh(center)
    return (center, residual, jnp.where(diagonal > 0, diagonal, 1.0), induced)


def statistics(own_residual, own_induced, cells, charge_terms):
    squares = jnp.sum(own_residual * own_residual)
    square_sum, charge_sum = lax.psum((squares, jnp.sum(own_induced)), ("gx", "gy", "gz"))
    charge_terms.append(charge_sum / cells)
    return jnp.sqrt(square_sum / cells + 1e-06)


def body(start_potential, permittivity, screening, source):
    shape = start_potential.shape
    cells = (
        shape[0]
        * shape[1]
        * shape[2]
        * lax.axis_size("gx")
        * lax.axis_size("gy")
        * lax.axis_size("gz")
    )
    norms = []
    charge_terms = []
    weights_pad = padded_2(permittivity, (("gx", 0), ("gy", 1), ("gz", 2)), 1)
    potential = start_potential
    for iteration in range(ITERS):
        padded = padded_2(potential, (("gx", 0), ("gy", 1), ("gz", 2)), 1)
        center, residual, diagonal, induced = relax(padded, weights_pad, screening, source)
        rms = statistics(residual, induced, cells, charge_terms)
        norms.append(rms)
        potential = center + 1.0 / (1.0 + rms) * residual / diagonal
    charges = jnp.stack(charge_terms)
    return (potential, jnp.stack(norms), charges)


def solution(mesh):
    placed = (P("gx", "gy", "gz"), P("gx", "gy", "gz"), P("gx", "gy", "gz"), P("gx", "gy", "gz"))
    return jax.shard_map(
        body, mesh=mesh, in_specs=placed, out_specs=(P("gx", "gy", "gz"), P(), P()), check_vma=False
    )
```

profile of v0, /device:TPU:0, one launch (start us, length us, event | category | flops | bytes accessed | tf_op | source)
XLA Modules:
  0.0 297.7 jit_solution(15585116569991222834)
XLA Ops:
  2.8 5.6 %collective-permute-start.2 = (f32[1,128,128]{2,0,1:T(1,128)S(1)}, f32[1,128,128]{2,0,1:T(1,128)S(1)}, u32[]{:S(2)}, u32[]{:S(2)}) collective-permute-start(f32[1,128,128]{2,0,1:T(1,128)S(1)} %bitcast.12), channel_id=1, source_target_pairs={{0,8},{8,16},{16,24},{1,9},{9,17},{17,25},{2,10},{10,18},{18,26},{... | collective-permute-start | bytes 196616 | tf_op jit(solution)/shard_map/ppermute | solution.py:16
  10.6 4.7 %collective-permute-start.3 = (f32[1,128,128]{2,0,1:T(1,128)S(1)}, f32[1,128,128]{2,0,1:T(1,128)S(1)}, u32[]{:S(2)}, u32[]{:S(2)}) collective-permute-start(f32[1,128,128]{2,0,1:T(1,128)S(1)} %bitcast.10), channel_id=1, source_target_pairs={{0,8},{8,16},{16,24},{1,9},{9,17},{17,25},{2,10},{10,18},{18,26},{... | collective-permute-start | bytes 196616 | tf_op jit(solution)/shard_map/ppermute | solution.py:16
  15.3 4.7 %fusion.88 = (f32[]{:T(128)}, f32[16,128,128]{2,0,1:T(8,128)}, f32[16,128,128]{2,0,1:T(8,128)S(1)}) fusion(f32[16,128,128]{2,1,0:T(8,128)} %param.4, f32[16,128,128]{2,1,0:T(8,128)} %param.6), kind=kLoop, calls=%fused_computation.203 | loop fusion | flops 3145727 | bytes 4194308 | tf_op jit(solution)/shard_map/reduce_sum | solution.py:55
  22.0 4.5 %collective-permute-start.6 = (f32[18,1,128]{2,0,1:T(8,128)S(1)}, f32[18,1,128]{2,0,1:T(8,128)S(1)}, u32[]{:S(2)}, u32[]{:S(2)}) collective-permute-start(f32[18,1,128]{2,0,1:T(8,128)S(1)} %get-tuple-element.44), channel_id=1, source_target_pairs={{0,4},{1,5},{2,6},{3,7},{8,12},{9,13},{10,14},{11,15},{16,20},{17,... | collective-permute-start | bytes 27656 | tf_op jit(solution)/shard_map/ppermute | solution.py:16
  31.6 2.4 copy.168
  34.0 2.4 copy.162
  37.6 3.0 %collective-permute-start.10 = (f32[18,130,1]{1,0,2:T(8,128)S(1)}, f32[18,130,1]{1,0,2:T(8,128)S(1)}, u32[]{:S(2)}, u32[]{:S(2)}) collective-permute-start(f32[18,130,1]{1,0,2:T(8,128)S(1)} %copy.168), channel_id=1, source_target_pairs={{0,1},{1,2},{2,3},{4,5},{5,6},{6,7},{8,9},{9,10},{10,11},{12,13},{... | collective-permute-start | bytes 28088 | tf_op jit(solution)/shard_map/ppermute | solution.py:16
  43.1 2.4 copy.165
  46.8 2.4 copy.171
  49.1 4.1 %collective-permute-start.11 = (f32[18,130,1]{1,0,2:T(8,128)S(1)}, f32[18,130,1]{1,0,2:T(8,128)S(1)}, u32[]{:S(2)}, u32[]{:S(2)}) collective-permute-start(f32[18,130,1]{1,0,2:T(8,128)S(1)} %copy.171), channel_id=1, source_target_pairs={{0,1},{1,2},{2,3},{4,5},{5,6},{6,7},{8,9},{9,10},{10,11},{12,13},{... | collective-permute-start | bytes 28088 | tf_op jit(solution)/shard_map/ppermute | solution.py:16
  61.7 9.7 %multiply_reduce_fusion.2 = (f32[]{:T(128)}, f32[16,128,128]{2,0,1:T(8,128)}, f32[16,128,128]{2,0,1:T(8,128)}, f32[16,128,128]{2,0,1:T(8,128)}) fusion(f32[16,128,128]{2,0,1:T(8,128)} %get-tuple-element.19, f32[16,128,128]{2,0,1:T(8,128)S(1)} %get-tuple-element.55, f32[18,1,128]{2,0,1:T(8,128)S(1)} %collective-permute-done.5, ...), kind=kLoop, calls=%fused_computation.183 | loop fusion | flops 23068672 | bytes 7676484 | tf_op jit(solution)/shard_map/reduce_sum | solution.py:54
  71.4 42.1 %psum.42 = f32[]{:T(128)} all-reduce(f32[]{:T(128)} %get-tuple-element.27), channel_id=1, replica_groups=mesh['gx'=4,'gy'=2,'gz'=4] {'gx','gy','gz'}, use_global_device_ids=true, to_apply=%region_1.2 | all-reduce | flops 1 | bytes 8 | tf_op jit(solution)/shard_map/psum | solution.py:55
  114.3 5.9 %fusion.16 = (f32[16,128,128]{2,0,1:T(8,128)S(1)}, f32[16,128,128]{2,0,1:T(8,128)}) fusion(f32[16,128,128]{2,0,1:T(8,128)} %get-tuple-element.28, f32[16,128,128]{2,1,0:T(8,128)S(1)} %copy-done, f32[]{:T(128)S(6)} %div.73, f32[16,128,128]{2,1,0:T(8,128)} %param.4, f32[16,128,128]{2,0,1:T(8,128)} %get-tuple-element.30, f32[16,128,128]{2,0,1:T(8,128)} %get-tuple-element.29, ...), kind=kLoop, calls=%fused_computation.32 | loop fusion | flops 11534336 | bytes 8538116 | tf_op jit(solution)/shard_map/add | solution.py:79
  124.3 4.3 %collective-permute-done.12 = f32[1,128,128]{2,0,1:T(1,128)S(1)} collective-permute-done((f32[1,128,128]{2,0,1:T(1,128)S(1)}, f32[1,128,128]{2,0,1:T(1,128)S(1)}, u32[]{:S(2)}, u32[]{:S(2)}) %collective-permute-start.12) | collective-permute-done | bytes 65568 | tf_op jit(solution)/shard_map/ppermute | solution.py:17
  128.6 4.2 %collective-permute-start.15 = (f32[18,1,128]{2,0,1:T(8,128)S(1)}, f32[18,1,128]{2,0,1:T(8,128)S(1)}, u32[]{:S(2)}, u32[]{:S(2)}) collective-permute-start(f32[18,1,128]{2,0,1:T(8,128)S(1)} %get-tuple-element.41), channel_id=1, source_target_pairs={{0,4},{1,5},{2,6},{3,7},{8,12},{9,13},{10,14},{11,15},{16,20},{17,... | collective-permute-start | bytes 27656 | tf_op jit(solution)/shard_map/ppermute | solution.py:16
  134.2 4.2 %collective-permute-done.14 = f32[18,1,128]{2,0,1:T(8,128)S(1)} collective-permute-done((f32[18,1,128]{2,0,1:T(8,128)S(1)}, f32[18,1,128]{2,0,1:T(8,128)S(1)}, u32[]{:S(2)}, u32[]{:S(2)}) %collective-permute-start.14) | collective-permute-done | bytes 9248 | tf_op jit(solution)/shard_map/ppermute | solution.py:17
  140.8 2.4 copy.182
  144.5 2.4 copy.184
  146.8 3.0 %collective-permute-start.17 = (f32[18,130,1]{1,0,2:T(8,128)S(1)}, f32[18,130,1]{1,0,2:T(8,128)S(1)}, u32[]{:S(2)}, u32[]{:S(2)}) collective-permute-start(f32[18,130,1]{1,0,2:T(8,128)S(1)} %copy.184), channel_id=1, source_target_pairs={{0,1},{1,2},{2,3},{4,5},{5,6},{6,7},{8,9},{9,10},{10,11},{12,13},{... | collective-permute-start | bytes 28088 | tf_op jit(solution)/shard_map/ppermute | solution.py:16
  154.1 8.9 %multiply_reduce_fusion.1 = (f32[]{:T(128)}, f32[16,128,128]{2,0,1:T(8,128)}) fusion(f32[16,128,128]{2,0,1:T(8,128)S(1)} %get-tuple-element.25, f32[16,128,128]{2,1,0:T(8,128)S(1)} %copy-done, f32[16,128,128]{2,0,1:T(8,128)} %get-tuple-element.30, f32[18,1,128]{2,0,1:T(8,128)S(1)} %collective-permute-done.14, ...), kind=kLoop, calls=%fused_computation.178 | loop fusion | flops 20709376 | bytes 7657764 | tf_op jit(solution)/shard_map/reduce_sum | solution.py:54
  163.0 39.6 %psum.43 = f32[]{:T(128)} all-reduce(f32[]{:T(128)} %get-tuple-element.23), channel_id=1, replica_groups=mesh['gx'=4,'gy'=2,'gz'=4] {'gx','gy','gz'}, use_global_device_ids=true, to_apply=%region_3.4 | all-reduce | flops 1 | bytes 8 | tf_op jit(solution)/shard_map/psum | solution.py:55
  203.3 4.5 %fusion.87 = (f32[]{:T(128)}, f32[]{:T(128)}, f32[16,128,128]{2,0,1:T(8,128)S(1)}) fusion(f32[16,128,128]{2,0,1:T(8,128)S(1)} %get-tuple-element.25, f32[16,128,128]{2,1,0:T(8,128)S(1)} %copy-done, f32[16,128,128]{2,0,1:T(8,128)} %get-tuple-element.26, f32[16,128,128]{2,0,1:T(8,128)} %get-tuple-element.24, f32[]{:T(128)S(6)} %div.76), kind=kLoop, calls=%fused_computation.202 | loop fusion | flops 8388606 | bytes 5242892 | tf_op jit(solution)/shard_map/reduce_sum | solution.py:55
  207.9 2.2 collective-permute-start.19
  212.0 4.3 %collective-permute-done.18 = f32[1,128,128]{2,0,1:T(1,128)S(1)} collective-permute-done((f32[1,128,128]{2,0,1:T(1,128)S(1)}, f32[1,128,128]{2,0,1:T(1,128)S(1)}, u32[]{:S(2)}, u32[]{:S(2)}) %collective-permute-start.18) | collective-permute-done | bytes 65568 | tf_op jit(solution)/shard_map/ppermute | solution.py:17
  216.3 4.2 %collective-permute-start.21 = (f32[18,1,128]{2,0,1:T(8,128)S(1)}, f32[18,1,128]{2,0,1:T(8,128)S(1)}, u32[]{:S(2)}, u32[]{:S(2)}) collective-permute-start(f32[18,1,128]{2,0,1:T(8,128)S(1)} %get-tuple-element.39), channel_id=1, source_target_pairs={{0,4},{1,5},{2,6},{3,7},{8,12},{9,13},{10,14},{11,15},{16,20},{17,... | collective-permute-start | bytes 27656 | tf_op jit(solution)/shard_map/ppermute | solution.py:16
  222.0 4.1 %collective-permute-done.20 = f32[18,1,128]{2,0,1:T(8,128)S(1)} collective-permute-done((f32[18,1,128]{2,0,1:T(8,128)S(1)}, f32[18,1,128]{2,0,1:T(8,128)S(1)}, u32[]{:S(2)}, u32[]{:S(2)}) %collective-permute-start.20) | collective-permute-done | bytes 9248 | tf_op jit(solution)/shard_map/ppermute | solution.py:17
  228.5 2.4 copy.189
  232.1 2.4 copy.191
  234.5 3.2 %collective-permute-start.23 = (f32[18,130,1]{1,0,2:T(8,128)S(1)}, f32[18,130,1]{1,0,2:T(8,128)S(1)}, u32[]{:S(2)}, u32[]{:S(2)}) collective-permute-start(f32[18,130,1]{1,0,2:T(8,128)S(1)} %copy.191), channel_id=1, source_target_pairs={{0,1},{1,2},{2,3},{4,5},{5,6},{6,7},{8,9},{9,10},{10,11},{12,13},{... | collective-permute-start | bytes 28088 | tf_op jit(solution)/shard_map/ppermute | solution.py:16
  241.9 8.9 %multiply_reduce_fusion = (f32[]{:T(128)}, f32[16,128,128]{2,0,1:T(8,128)}) fusion(f32[16,128,128]{2,0,1:T(8,128)S(1)} %copy-done.2, f32[16,128,128]{2,1,0:T(8,128)S(1)} %copy-done, f32[16,128,128]{2,0,1:T(8,128)} %get-tuple-element.30, f32[18,1,128]{2,0,1:T(8,128)S(1)} %collective-permute-done.20, f32[1,128,128]{2,0,1:T(1,128)S(1)} %collective-permute-done.18, ...), kind=kLoop, calls=%fused_computation.174 | loop fusion | flops 20709376 | bytes 7657764 | tf_op jit(solution)/shard_map/reduce_sum | solution.py:54
  250.8 39.9 %all-reduce = (f32[]{:T(128)}, f32[]{:T(128)}, f32[]{:T(128)}, f32[]{:T(128)}) all-reduce(f32[]{:T(128)} %get-tuple-element.21, f32[]{:T(128)} %get-tuple-element.13, f32[]{:T(128)} %get-tuple-element.12, f32[]{:T(128)} %get-tuple-element.18), channel_id=1, replica_groups=mesh['gx'=4,'gy'=2,'gz'=4] {'gx','gy','gz'}, use_global_device_ids=true, to_apply=%region_5.6 | all-reduce | flops 4 | bytes 32 | tf_op jit(solution)/shard_map/psum | solution.py:55
  293.3 2.5 fusion.20
  (69 shorter events, 51.4 us)
Async XLA Ops:
  1.5 19.1 %collective-permute-start = (f32[1,128,128]{2,0,1:T(1,128)S(1)}, f32[1,128,128]{2,0,1:T(1,128)S(1)}, u32[]{:S(2)}, u32[]{:S(2)}) collective-permute-start(f32[1,128,128]{2,0,1:T(1,128)S(1)} %bitcast.13), channel_id=1, source_target_pairs={{8,0},{16,8},{24,16},{9,1},{17,9},{25,17},{10,2},{18,10},{26,18},{... | collective-permute-start | bytes 196616 | tf_op jit(solution)/shard_map/ppermute | solution.py:17
  2.8 17.9 %collective-permute-start.2 = (f32[1,128,128]{2,0,1:T(1,128)S(1)}, f32[1,128,128]{2,0,1:T(1,128)S(1)}, u32[]{:S(2)}, u32[]{:S(2)}) collective-permute-start(f32[1,128,128]{2,0,1:T(1,128)S(1)} %bitcast.12), channel_id=1, source_target_pairs={{0,8},{8,16},{16,24},{1,9},{9,17},{17,25},{2,10},{10,18},{18,26},{... | collective-permute-start | bytes 196616 | tf_op jit(solution)/shard_map/ppermute | solution.py:16
  9.3 17.3 %collective-permute-start.1 = (f32[1,128,128]{2,0,1:T(1,128)S(1)}, f32[1,128,128]{2,0,1:T(1,128)S(1)}, u32[]{:S(2)}, u32[]{:S(2)}) collective-permute-start(f32[1,128,128]{2,0,1:T(1,128)S(1)} %bitcast.11), channel_id=1, source_target_pairs={{8,0},{16,8},{24,16},{9,1},{17,9},{25,17},{10,2},{18,10},{26,18},{... | collective-permute-start | bytes 196616 | tf_op jit(solution)/shard_map/ppermute | solution.py:17
  10.6 9.4 %copy-start.3 = (f32[16,128,128]{2,1,0:T(8,128)S(1)}, f32[16,128,128]{2,1,0:T(8,128)}, u32[]{:S(2)}) copy-start(f32[16,128,128]{2,1,0:T(8,128)} %param.5) | copy-start | bytes 3145732
  10.6 16.0 %collective-permute-start.3 = (f32[1,128,128]{2,0,1:T(1,128)S(1)}, f32[1,128,128]{2,0,1:T(1,128)S(1)}, u32[]{:S(2)}, u32[]{:S(2)}) collective-permute-start(f32[1,128,128]{2,0,1:T(1,128)S(1)} %bitcast.10), channel_id=1, source_target_pairs={{0,8},{8,16},{16,24},{1,9},{9,17},{17,25},{2,10},{10,18},{18,26},{... | collective-permute-start | bytes 196616 | tf_op jit(solution)/shard_map/ppermute | solution.py:16
  20.7 8.5 %collective-permute-start.4 = (f32[18,1,128]{2,0,1:T(8,128)S(1)}, f32[18,1,128]{2,0,1:T(8,128)S(1)}, u32[]{:S(2)}, u32[]{:S(2)}) collective-permute-start(f32[18,1,128]{2,0,1:T(8,128)S(1)} %get-tuple-element.43), channel_id=1, source_target_pairs={{4,0},{5,1},{6,2},{7,3},{12,8},{13,9},{14,10},{15,11},{20,16},{21,... | collective-permute-start | bytes 27656 | tf_op jit(solution)/shard_map/ppermute | solution.py:17
  22.0 7.2 %collective-permute-start.6 = (f32[18,1,128]{2,0,1:T(8,128)S(1)}, f32[18,1,128]{2,0,1:T(8,128)S(1)}, u32[]{:S(2)}, u32[]{:S(2)}) collective-permute-start(f32[18,1,128]{2,0,1:T(8,128)S(1)} %get-tuple-element.44), channel_id=1, source_target_pairs={{0,4},{1,5},{2,6},{3,7},{8,12},{9,13},{10,14},{11,15},{16,20},{17,... | collective-permute-start | bytes 27656 | tf_op jit(solution)/shard_map/ppermute | solution.py:16
  26.6 14.1 %collective-permute-start.7 = (f32[18,1,128]{2,0,1:T(8,128)S(1)}, f32[18,1,128]{2,0,1:T(8,128)S(1)}, u32[]{:S(2)}, u32[]{:S(2)}) collective-permute-start(f32[18,1,128]{2,0,1:T(8,128)S(1)} %get-tuple-element.45), channel_id=1, source_target_pairs={{0,4},{1,5},{2,6},{3,7},{8,12},{9,13},{10,14},{11,15},{16,20},{17,... | collective-permute-start | bytes 27656 | tf_op jit(solution)/shard_map/ppermute | solution.py:16
  27.9 12.8 %collective-permute-start.5 = (f32[18,1,128]{2,0,1:T(8,128)S(1)}, f32[18,1,128]{2,0,1:T(8,128)S(1)}, u32[]{:S(2)}, u32[]{:S(2)}) collective-permute-start(f32[18,1,128]{2,0,1:T(8,128)S(1)} %get-tuple-element.46), channel_id=1, source_target_pairs={{4,0},{5,1},{6,2},{7,3},{12,8},{13,9},{14,10},{15,11},{20,16},{21,... | collective-permute-start | bytes 27656 | tf_op jit(solution)/shard_map/ppermute | solution.py:17
  36.3 19.1 %collective-permute-start.8 = (f32[18,130,1]{1,0,2:T(8,128)S(1)}, f32[18,130,1]{1,0,2:T(8,128)S(1)}, u32[]{:S(2)}, u32[]{:S(2)}) collective-permute-start(f32[18,130,1]{1,0,2:T(8,128)S(1)} %copy.162), channel_id=1, source_target_pairs={{1,0},{2,1},{3,2},{5,4},{6,5},{7,6},{9,8},{10,9},{11,10},{13,12},{... | collective-permute-start | bytes 28088 | tf_op jit(solution)/shard_map/ppermute | solution.py:17
  37.6 15.6 %collective-permute-start.10 = (f32[18,130,1]{1,0,2:T(8,128)S(1)}, f32[18,130,1]{1,0,2:T(8,128)S(1)}, u32[]{:S(2)}, u32[]{:S(2)}) collective-permute-start(f32[18,130,1]{1,0,2:T(8,128)S(1)} %copy.168), channel_id=1, source_target_pairs={{0,1},{1,2},{2,3},{4,5},{5,6},{6,7},{8,9},{9,10},{10,11},{12,13},{... | collective-permute-start | bytes 28088 | tf_op jit(solution)/shard_map/ppermute | solution.py:16
  45.5 12.1 %collective-permute-start.9 = (f32[18,130,1]{1,0,2:T(8,128)S(1)}, f32[18,130,1]{1,0,2:T(8,128)S(1)}, u32[]{:S(2)}, u32[]{:S(2)}) collective-permute-start(f32[18,130,1]{1,0,2:T(8,128)S(1)} %copy.165), channel_id=1, source_target_pairs={{1,0},{2,1},{3,2},{5,4},{6,5},{7,6},{9,8},{10,9},{11,10},{13,12},{... | collective-permute-start | bytes 28088 | tf_op jit(solution)/shard_map/ppermute | solution.py:17
  49.1 10.5 %collective-permute-start.11 = (f32[18,130,1]{1,0,2:T(8,128)S(1)}, f32[18,130,1]{1,0,2:T(8,128)S(1)}, u32[]{:S(2)}, u32[]{:S(2)}) collective-permute-start(f32[18,130,1]{1,0,2:T(8,128)S(1)} %copy.171), channel_id=1, source_target_pairs={{0,1},{1,2},{2,3},{4,5},{5,6},{6,7},{8,9},{9,10},{10,11},{12,13},{... | collective-permute-start | bytes 28088 | tf_op jit(solution)/shard_map/ppermute | solution.py:16
  61.7 52.6 %copy-start = (f32[16,128,128]{2,1,0:T(8,128)S(1)}, f32[16,128,128]{2,1,0:T(8,128)}, u32[]{:S(2)}) copy-start(f32[16,128,128]{2,1,0:T(8,128)} %param.6) | copy-start | bytes 3145732
  120.3 4.0 %collective-permute-start.13 = (f32[1,128,128]{2,0,1:T(1,128)S(1)}, f32[1,128,128]{2,0,1:T(1,128)S(1)}, u32[]{:S(2)}, u32[]{:S(2)}) collective-permute-start(f32[1,128,128]{2,0,1:T(1,128)S(1)} %get-tuple-element.49), channel_id=1, source_target_pairs={{0,8},{8,16},{16,24},{1,9},{9,17},{17,25},{2,10},{10,18},{18,26},{... | collective-permute-start | bytes 196616 | tf_op jit(solution)/shard_map/ppermute | solution.py:16
  122.4 6.2 %collective-permute-start.12 = (f32[1,128,128]{2,0,1:T(1,128)S(1)}, f32[1,128,128]{2,0,1:T(1,128)S(1)}, u32[]{:S(2)}, u32[]{:S(2)}) collective-permute-start(f32[1,128,128]{2,0,1:T(1,128)S(1)} %get-tuple-element.50), channel_id=1, source_target_pairs={{8,0},{16,8},{24,16},{9,1},{17,9},{25,17},{10,2},{18,10},{26,18},{... | collective-permute-start | bytes 196616 | tf_op jit(solution)/shard_map/ppermute | solution.py:17
  128.6 5.6 %collective-permute-start.15 = (f32[18,1,128]{2,0,1:T(8,128)S(1)}, f32[18,1,128]{2,0,1:T(8,128)S(1)}, u32[]{:S(2)}, u32[]{:S(2)}) collective-permute-start(f32[18,1,128]{2,0,1:T(8,128)S(1)} %get-tuple-element.41), channel_id=1, source_target_pairs={{0,4},{1,5},{2,6},{3,7},{8,12},{9,13},{10,14},{11,15},{16,20},{17,... | collective-permute-start | bytes 27656 | tf_op jit(solution)/shard_map/ppermute | solution.py:16
  132.8 5.6 %collective-permute-start.14 = (f32[18,1,128]{2,0,1:T(8,128)S(1)}, f32[18,1,128]{2,0,1:T(8,128)S(1)}, u32[]{:S(2)}, u32[]{:S(2)}) collective-permute-start(f32[18,1,128]{2,0,1:T(8,128)S(1)} %get-tuple-element.42), channel_id=1, source_target_pairs={{4,0},{5,1},{6,2},{7,3},{12,8},{13,9},{14,10},{15,11},{20,16},{21,... | collective-permute-start | bytes 27656 | tf_op jit(solution)/shard_map/ppermute | solution.py:17
  143.2 6.7 %collective-permute-start.16 = (f32[18,130,1]{1,0,2:T(8,128)S(1)}, f32[18,130,1]{1,0,2:T(8,128)S(1)}, u32[]{:S(2)}, u32[]{:S(2)}) collective-permute-start(f32[18,130,1]{1,0,2:T(8,128)S(1)} %copy.182), channel_id=1, source_target_pairs={{1,0},{2,1},{3,2},{5,4},{6,5},{7,6},{9,8},{10,9},{11,10},{13,12},{... | collective-permute-start | bytes 28088 | tf_op jit(solution)/shard_map/ppermute | solution.py:17
  146.8 5.1 %collective-permute-start.17 = (f32[18,130,1]{1,0,2:T(8,128)S(1)}, f32[18,130,1]{1,0,2:T(8,128)S(1)}, u32[]{:S(2)}, u32[]{:S(2)}) collective-permute-start(f32[18,130,1]{1,0,2:T(8,128)S(1)} %copy.184), channel_id=1, source_target_pairs={{0,1},{1,2},{2,3},{4,5},{5,6},{6,7},{8,9},{9,10},{10,11},{12,13},{... | collective-permute-start | bytes 28088 | tf_op jit(solution)/shard_map/ppermute | solution.py:16
  207.8 18.3 %copy-start.1 = (f32[16,128,128]{2,0,1:T(8,128)}, f32[16,128,128]{2,0,1:T(8,128)S(1)}, u32[]{:S(2)}) copy-start(f32[16,128,128]{2,0,1:T(8,128)S(1)} %get-tuple-element.20) | copy-start | bytes 3145732
  207.9 4.1 %collective-permute-start.19 = (f32[1,128,128]{2,0,1:T(1,128)S(1)}, f32[1,128,128]{2,0,1:T(1,128)S(1)}, u32[]{:S(2)}, u32[]{:S(2)}) collective-permute-start(f32[1,128,128]{2,0,1:T(1,128)S(1)} %get-tuple-element.47), channel_id=1, source_target_pairs={{0,8},{8,16},{16,24},{1,9},{9,17},{17,25},{2,10},{10,18},{18,26},{... | collective-permute-start | bytes 196616 | tf_op jit(solution)/shard_map/ppermute | solution.py:16
  210.1 6.2 %collective-permute-start.18 = (f32[1,128,128]{2,0,1:T(1,128)S(1)}, f32[1,128,128]{2,0,1:T(1,128)S(1)}, u32[]{:S(2)}, u32[]{:S(2)}) collective-permute-start(f32[1,128,128]{2,0,1:T(1,128)S(1)} %get-tuple-element.48), channel_id=1, source_target_pairs={{8,0},{16,8},{24,16},{9,1},{17,9},{25,17},{10,2},{18,10},{26,18},{... | collective-permute-start | bytes 196616 | tf_op jit(solution)/shard_map/ppermute | solution.py:17
  216.3 5.7 %collective-permute-start.21 = (f32[18,1,128]{2,0,1:T(8,128)S(1)}, f32[18,1,128]{2,0,1:T(8,128)S(1)}, u32[]{:S(2)}, u32[]{:S(2)}) collective-permute-start(f32[18,1,128]{2,0,1:T(8,128)S(1)} %get-tuple-element.39), channel_id=1, source_target_pairs={{0,4},{1,5},{2,6},{3,7},{8,12},{9,13},{10,14},{11,15},{16,20},{17,... | collective-permute-start | bytes 27656 | tf_op jit(solution)/shard_map/ppermute | solution.py:16
  220.5 5.6 %collective-permute-start.20 = (f32[18,1,128]{2,0,1:T(8,128)S(1)}, f32[18,1,128]{2,0,1:T(8,128)S(1)}, u32[]{:S(2)}, u32[]{:S(2)}) collective-permute-start(f32[18,1,128]{2,0,1:T(8,128)S(1)} %get-tuple-element.40), channel_id=1, source_target_pairs={{4,0},{5,1},{6,2},{7,3},{12,8},{13,9},{14,10},{15,11},{20,16},{21,... | collective-permute-start | bytes 27656 | tf_op jit(solution)/shard_map/ppermute | solution.py:17
  230.8 6.8 %collective-permute-start.22 = (f32[18,130,1]{1,0,2:T(8,128)S(1)}, f32[18,130,1]{1,0,2:T(8,128)S(1)}, u32[]{:S(2)}, u32[]{:S(2)}) collective-permute-start(f32[18,130,1]{1,0,2:T(8,128)S(1)} %copy.189), channel_id=1, source_target_pairs={{1,0},{2,1},{3,2},{5,4},{6,5},{7,6},{9,8},{10,9},{11,10},{13,12},{... | collective-permute-start | bytes 28088 | tf_op jit(solution)/shard_map/ppermute | solution.py:17
  234.5 7.4 %copy-start.2 = (f32[16,128,128]{2,0,1:T(8,128)S(1)}, f32[16,128,128]{2,0,1:T(8,128)}, u32[]{:S(2)}) copy-start(f32[16,128,128]{2,0,1:T(8,128)} %copy-done.1) | copy-start | bytes 3145732
  234.5 5.3 %collective-permute-start.23 = (f32[18,130,1]{1,0,2:T(8,128)S(1)}, f32[18,130,1]{1,0,2:T(8,128)S(1)}, u32[]{:S(2)}, u32[]{:S(2)}) collective-permute-start(f32[18,130,1]{1,0,2:T(8,128)S(1)} %copy.191), channel_id=1, source_target_pairs={{0,1},{1,2},{2,3},{4,5},{5,6},{6,7},{8,9},{9,10},{10,11},{12,13},{... | collective-permute-start | bytes 28088 | tf_op jit(solution)/shard_map/ppermute | solution.py:16
where the time goes:
time: 299 us; the launch traced here: 298 us
  blocking collectives  122 us (41%)
  starting transfers between devices  57.9 us (19%)
  local copies, waits for them, and re-layouts  48.2 us (16%)
  other arithmetic  46.6 us (16%)
  waiting for transfers between devices  18.1 us (6%)
  between operations  5.17 us (2%)
    psum x3, blocking collectives, statistics(): lax.psum((squares, jnp.sum(own_induced)), ('gx', 'gy', 'gz'))  122 us
    ppermute x12, starting transfers between devices, padded_2(): before = lax.ppermute(last, axis, up)  42.2 us
    reduce_sum x3, other arithmetic, statistics(): squares = jnp.sum(own_residual * own_residual)  27.5 us
    ppermute x12, waiting for transfers between devices, padded_2(): after = lax.ppermute(initial, axis, down)  16.8 us
    slice x7, local copies, waits for them, and re-layouts, padded_2(): initial = lax.slice_in_dim(array, 0, width, axis=dim)  15.9 us
    ppermute x12, starting transfers between devices, padded_2(): after = lax.ppermute(initial, axis, down)  15.7 us
    slice x9, local copies, waits for them, and re-layouts, padded_2(): last = lax.slice_in_dim(array, length - width, length, axis=dim)  13.5 us
    reduce_sum x2, other arithmetic, statistics(): jnp.sum(own_induced)  9.21 us
  transfers between devices with their start and end apart: 24, of which 7 were waited for; matrix products, arithmetic and copies ran while one was open for 12% of the time, Pallas kernels for 0%

commit v1 on v0

--- a/solution.py
+++ b/solution.py
@@ -52,7 +52,7 @@
 
 def statistics(own_residual, own_induced, cells, charge_terms):
     squares = jnp.sum(own_residual * own_residual)
-    square_sum, charge_sum = lax.psum((squares, jnp.sum(own_induced)), ("gx", "gy", "gz"))
+    square_sum, charge_sum = lax.psum(lax.psum((squares, jnp.sum(own_induced)), ("gy", "gz")), "gx")
     charge_terms.append(charge_sum / cells)
     return jnp.sqrt(square_sum / cells + 1e-06)
 

time: 299 us -> 246 us (0.82)
  blocking collectives: 122 us -> 68.3 us
    psum x3 -> x6, blocking collectives: 122 us -> 68.3 us  [the longest x3 39.6 us: statistics(): lax.psum((squares, jnp.sum(own_induced)), ('gy', 'gz'))]
  transfers between devices with their start and end apart: 24 -> 24, of which waited for: 7 -> 8; matrix products, arithmetic and copies ran while one was open for 12% -> 15% of each run, Pallas kernels for 0% -> 0%
where the time goes in v1:
time: 246 us; the launch traced here: 244 us
  blocking collectives  68.3 us (28%)
  starting transfers between devices  57.9 us (24%)
  local copies, waits for them, and re-layouts  48.3 us (20%)
  other arithmetic  46.6 us (19%)
  waiting for transfers between devices  18.3 us (7%)
  between operations  5.03 us (2%)
    ppermute x12, starting transfers between devices, padded_2(): before = lax.ppermute(last, axis, up)  42.2 us
    psum x3, blocking collectives, statistics(): lax.psum((squares, jnp.sum(own_induced)), ('gy', 'gz'))  39.6 us
    psum x3, blocking collectives, statistics(): lax.psum(lax.psum((squares, jnp.sum(own_induced)), ('gy', 'gz')), 'gx')  28.7 us
    reduce_sum x3, other arithmetic, statistics(): squares = jnp.sum(own_residual * own_residual)  27.5 us
    ppermute x12, waiting for transfers between devices, padded_2(): after = lax.ppermute(initial, axis, down)  17 us
    slice x7, local copies, waits for them, and re-layouts, padded_2(): initial = lax.slice_in_dim(array, 0, width, axis=dim)  15.9 us
    ppermute x12, starting transfers between devices, padded_2(): after = lax.ppermute(initial, axis, down)  15.7 us
    slice x9, local copies, waits for them, and re-layouts, padded_2(): last = lax.slice_in_dim(array, length - width, length, axis=dim)  13.6 us
  transfers between devices with their start and end apart: 24, of which 8 were waited for; matrix products, arithmetic and copies ran while one was open for 15% of the time, Pallas kernels for 0%

profile of v1, /device:TPU:0, one launch (start us, length us, event | category | flops | bytes accessed | tf_op | source)
XLA Modules:
  0.0 244.5 jit_solution(13689367467582343824)
XLA Ops:
  2.8 5.6 %collective-permute-start.2 = (f32[1,128,128]{2,0,1:T(1,128)S(1)}, f32[1,128,128]{2,0,1:T(1,128)S(1)}, u32[]{:S(2)}, u32[]{:S(2)}) collective-permute-start(f32[1,128,128]{2,0,1:T(1,128)S(1)} %bitcast.12), channel_id=1, source_target_pairs={{0,8},{8,16},{16,24},{1,9},{9,17},{17,25},{2,10},{10,18},{18,26},{... | collective-permute-start | bytes 196616 | tf_op jit(solution)/shard_map/ppermute | solution.py:16
  10.6 4.7 %collective-permute-start.3 = (f32[1,128,128]{2,0,1:T(1,128)S(1)}, f32[1,128,128]{2,0,1:T(1,128)S(1)}, u32[]{:S(2)}, u32[]{:S(2)}) collective-permute-start(f32[1,128,128]{2,0,1:T(1,128)S(1)} %bitcast.10), channel_id=1, source_target_pairs={{0,8},{8,16},{16,24},{1,9},{9,17},{17,25},{2,10},{10,18},{18,26},{... | collective-permute-start | bytes 196616 | tf_op jit(solution)/shard_map/ppermute | solution.py:16
  15.3 4.7 %fusion.88 = (f32[]{:T(128)}, f32[16,128,128]{2,0,1:T(8,128)}, f32[16,128,128]{2,0,1:T(8,128)S(1)}) fusion(f32[16,128,128]{2,1,0:T(8,128)} %param.4, f32[16,128,128]{2,1,0:T(8,128)} %param.6), kind=kLoop, calls=%fused_computation.203 | loop fusion | flops 3145727 | bytes 4194308 | tf_op jit(solution)/shard_map/reduce_sum | solution.py:55
  22.0 4.5 %collective-permute-start.6 = (f32[18,1,128]{2,0,1:T(8,128)S(1)}, f32[18,1,128]{2,0,1:T(8,128)S(1)}, u32[]{:S(2)}, u32[]{:S(2)}) collective-permute-start(f32[18,1,128]{2,0,1:T(8,128)S(1)} %get-tuple-element.48), channel_id=1, source_target_pairs={{0,4},{1,5},{2,6},{3,7},{8,12},{9,13},{10,14},{11,15},{16,20},{17,... | collective-permute-start | bytes 27656 | tf_op jit(solution)/shard_map/ppermute | solution.py:16
  34.0 2.4 copy.162
  37.7 3.0 %collective-permute-start.10 = (f32[18,130,1]{1,0,2:T(8,128)S(1)}, f32[18,130,1]{1,0,2:T(8,128)S(1)}, u32[]{:S(2)}, u32[]{:S(2)}) collective-permute-start(f32[18,130,1]{1,0,2:T(8,128)S(1)} %copy.168), channel_id=1, source_target_pairs={{0,1},{1,2},{2,3},{4,5},{5,6},{6,7},{8,9},{9,10},{10,11},{12,13},{... | collective-permute-start | bytes 28088 | tf_op jit(solution)/shard_map/ppermute | solution.py:16
  43.1 2.4 copy.165
  46.8 2.4 copy.171
  49.2 4.1 %collective-permute-start.11 = (f32[18,130,1]{1,0,2:T(8,128)S(1)}, f32[18,130,1]{1,0,2:T(8,128)S(1)}, u32[]{:S(2)}, u32[]{:S(2)}) collective-permute-start(f32[18,130,1]{1,0,2:T(8,128)S(1)} %copy.171), channel_id=1, source_target_pairs={{0,1},{1,2},{2,3},{4,5},{5,6},{6,7},{8,9},{9,10},{10,11},{12,13},{... | collective-permute-start | bytes 28088 | tf_op jit(solution)/shard_map/ppermute | solution.py:16
  61.8 9.7 %multiply_reduce_fusion.2 = (f32[]{:T(128)}, f32[16,128,128]{2,0,1:T(8,128)}, f32[16,128,128]{2,0,1:T(8,128)}, f32[16,128,128]{2,0,1:T(8,128)}) fusion(f32[16,128,128]{2,0,1:T(8,128)} %get-tuple-element.23, f32[16,128,128]{2,0,1:T(8,128)S(1)} %get-tuple-element.59, f32[18,1,128]{2,0,1:T(8,128)S(1)} %collective-permute-done.5, ...), kind=kLoop, calls=%fused_computation.183 | loop fusion | flops 23068672 | bytes 7676484 | tf_op jit(solution)/shard_map/reduce_sum | solution.py:54
  71.5 14.7 %psum.84 = f32[]{:T(128)} all-reduce(f32[]{:T(128)} %get-tuple-element.31), channel_id=1, replica_groups=mesh['gx'=4,'gy'=2,'gz'=4] {'gy','gz'}, use_global_device_ids=true, to_apply=%region_1.2 | all-reduce | flops 1 | bytes 8 | tf_op jit(solution)/shard_map/psum | solution.py:55
  86.1 10.7 %psum.85 = f32[]{:T(128)} all-reduce(f32[]{:T(128)} %psum.84), channel_id=1, replica_groups=mesh['gx'=4,'gy'=2,'gz'=4] {'gx'}, use_global_device_ids=true, to_apply=%region_2.3 | all-reduce | flops 1 | bytes 8 | tf_op jit(solution)/shard_map/psum | solution.py:55
  97.6 5.9 %fusion.16 = (f32[16,128,128]{2,0,1:T(8,128)S(1)}, f32[16,128,128]{2,0,1:T(8,128)}) fusion(f32[16,128,128]{2,0,1:T(8,128)} %get-tuple-element.32, f32[16,128,128]{2,1,0:T(8,128)S(1)} %copy-done, f32[]{:T(128)S(6)} %div.73, f32[16,128,128]{2,1,0:T(8,128)} %param.4, f32[16,128,128]{2,0,1:T(8,128)} %get-tuple-element.34, f32[16,128,128]{2,0,1:T(8,128)} %get-tuple-element.33, ...), kind=kLoop, calls=%fused_computation.32 | loop fusion | flops 11534336 | bytes 8538116 | tf_op jit(solution)/shard_map/add | solution.py:79
  103.6 2.5 %collective-permute-start.13 = (f32[1,128,128]{2,0,1:T(1,128)S(1)}, f32[1,128,128]{2,0,1:T(1,128)S(1)}, u32[]{:S(2)}, u32[]{:S(2)}) collective-permute-start(f32[1,128,128]{2,0,1:T(1,128)S(1)} %get-tuple-element.53), channel_id=1, source_target_pairs={{0,8},{8,16},{16,24},{1,9},{9,17},{17,25},{2,10},{10,18},{18,26},{... | collective-permute-start | bytes 196616 | tf_op jit(solution)/shard_map/ppermute | solution.py:16
  108.0 4.3 %collective-permute-done.12 = f32[1,128,128]{2,0,1:T(1,128)S(1)} collective-permute-done((f32[1,128,128]{2,0,1:T(1,128)S(1)}, f32[1,128,128]{2,0,1:T(1,128)S(1)}, u32[]{:S(2)}, u32[]{:S(2)}) %collective-permute-start.12) | collective-permute-done | bytes 65568 | tf_op jit(solution)/shard_map/ppermute | solution.py:17
  112.3 4.0 %collective-permute-start.15 = (f32[18,1,128]{2,0,1:T(8,128)S(1)}, f32[18,1,128]{2,0,1:T(8,128)S(1)}, u32[]{:S(2)}, u32[]{:S(2)}) collective-permute-start(f32[18,1,128]{2,0,1:T(8,128)S(1)} %get-tuple-element.45), channel_id=1, source_target_pairs={{0,4},{1,5},{2,6},{3,7},{8,12},{9,13},{10,14},{11,15},{16,20},{17,... | collective-permute-start | bytes 27656 | tf_op jit(solution)/shard_map/ppermute | solution.py:16
  117.7 4.2 %collective-permute-done.14 = f32[18,1,128]{2,0,1:T(8,128)S(1)} collective-permute-done((f32[18,1,128]{2,0,1:T(8,128)S(1)}, f32[18,1,128]{2,0,1:T(8,128)S(1)}, u32[]{:S(2)}, u32[]{:S(2)}) %collective-permute-start.14) | collective-permute-done | bytes 9248 | tf_op jit(solution)/shard_map/ppermute | solution.py:17
  128.0 2.4 copy.184
  130.3 3.0 %collective-permute-start.17 = (f32[18,130,1]{1,0,2:T(8,128)S(1)}, f32[18,130,1]{1,0,2:T(8,128)S(1)}, u32[]{:S(2)}, u32[]{:S(2)}) collective-permute-start(f32[18,130,1]{1,0,2:T(8,128)S(1)} %copy.184), channel_id=1, source_target_pairs={{0,1},{1,2},{2,3},{4,5},{5,6},{6,7},{8,9},{9,10},{10,11},{12,13},{... | collective-permute-start | bytes 28088 | tf_op jit(solution)/shard_map/ppermute | solution.py:16
  137.6 8.9 %multiply_reduce_fusion.1 = (f32[]{:T(128)}, f32[16,128,128]{2,0,1:T(8,128)}) fusion(f32[16,128,128]{2,0,1:T(8,128)S(1)} %get-tuple-element.29, f32[16,128,128]{2,1,0:T(8,128)S(1)} %copy-done, f32[16,128,128]{2,0,1:T(8,128)} %get-tuple-element.34, f32[18,1,128]{2,0,1:T(8,128)S(1)} %collective-permute-done.14, ...), kind=kLoop, calls=%fused_computation.178 | loop fusion | flops 20709376 | bytes 7657764 | tf_op jit(solution)/shard_map/reduce_sum | solution.py:54
  146.4 12.4 %psum.86 = f32[]{:T(128)} all-reduce(f32[]{:T(128)} %get-tuple-element.27), channel_id=1, replica_groups=mesh['gx'=4,'gy'=2,'gz'=4] {'gy','gz'}, use_global_device_ids=true, to_apply=%region_4.5 | all-reduce | flops 1 | bytes 8 | tf_op jit(solution)/shard_map/psum | solution.py:55
  158.9 9.0 %psum.87 = f32[]{:T(128)} all-reduce(f32[]{:T(128)} %psum.86), channel_id=1, replica_groups=mesh['gx'=4,'gy'=2,'gz'=4] {'gx'}, use_global_device_ids=true, to_apply=%region_5.6 | all-reduce | flops 1 | bytes 8 | tf_op jit(solution)/shard_map/psum | solution.py:55
  168.6 4.4 %fusion.87 = (f32[]{:T(128)}, f32[]{:T(128)}, f32[16,128,128]{2,0,1:T(8,128)S(1)}) fusion(f32[16,128,128]{2,0,1:T(8,128)S(1)} %get-tuple-element.29, f32[16,128,128]{2,1,0:T(8,128)S(1)} %copy-done, f32[16,128,128]{2,0,1:T(8,128)} %get-tuple-element.30, f32[16,128,128]{2,0,1:T(8,128)} %get-tuple-element.28, f32[]{:T(128)S(6)} %div.76), kind=kLoop, calls=%fused_computation.202 | loop fusion | flops 8388606 | bytes 5242892 | tf_op jit(solution)/shard_map/reduce_sum | solution.py:55
  173.1 3.9 %collective-permute-start.19 = (f32[1,128,128]{2,0,1:T(1,128)S(1)}, f32[1,128,128]{2,0,1:T(1,128)S(1)}, u32[]{:S(2)}, u32[]{:S(2)}) collective-permute-start(f32[1,128,128]{2,0,1:T(1,128)S(1)} %get-tuple-element.51), channel_id=1, source_target_pairs={{0,8},{8,16},{16,24},{1,9},{9,17},{17,25},{2,10},{10,18},{18,26},{... | collective-permute-start | bytes 196616 | tf_op jit(solution)/shard_map/ppermute | solution.py:16
  178.9 4.3 %collective-permute-done.18 = f32[1,128,128]{2,0,1:T(1,128)S(1)} collective-permute-done((f32[1,128,128]{2,0,1:T(1,128)S(1)}, f32[1,128,128]{2,0,1:T(1,128)S(1)}, u32[]{:S(2)}, u32[]{:S(2)}) %collective-permute-start.18) | collective-permute-done | bytes 65568 | tf_op jit(solution)/shard_map/ppermute | solution.py:17
  186.9 4.2 %collective-permute-done.20 = f32[18,1,128]{2,0,1:T(8,128)S(1)} collective-permute-done((f32[18,1,128]{2,0,1:T(8,128)S(1)}, f32[18,1,128]{2,0,1:T(8,128)S(1)}, u32[]{:S(2)}, u32[]{:S(2)}) %collective-permute-start.20) | collective-permute-done | bytes 9248 | tf_op jit(solution)/shard_map/ppermute | solution.py:17
  197.4 2.4 copy.191
  199.8 3.2 %collective-permute-start.23 = (f32[18,130,1]{1,0,2:T(8,128)S(1)}, f32[18,130,1]{1,0,2:T(8,128)S(1)}, u32[]{:S(2)}, u32[]{:S(2)}) collective-permute-start(f32[18,130,1]{1,0,2:T(8,128)S(1)} %copy.191), channel_id=1, source_target_pairs={{0,1},{1,2},{2,3},{4,5},{5,6},{6,7},{8,9},{9,10},{10,11},{12,13},{... | collective-permute-start | bytes 28088 | tf_op jit(solution)/shard_map/ppermute | solution.py:16
  207.2 8.9 %multiply_reduce_fusion = (f32[]{:T(128)}, f32[16,128,128]{2,0,1:T(8,128)}) fusion(f32[16,128,128]{2,0,1:T(8,128)S(1)} %copy-done.2, f32[16,128,128]{2,1,0:T(8,128)S(1)} %copy-done, f32[16,128,128]{2,0,1:T(8,128)} %get-tuple-element.34, f32[18,1,128]{2,0,1:T(8,128)S(1)} %collective-permute-done.20, f32[1,128,128]{2,0,1:T(1,128)S(1)} %collective-permute-done.18, ...), kind=kLoop, calls=%fused_computation.174 | loop fusion | flops 20709376 | bytes 7657764 | tf_op jit(solution)/shard_map/reduce_sum | solution.py:54
  216.1 12.5 %all-reduce = (f32[]{:T(128)}, f32[]{:T(128)}, f32[]{:T(128)}, f32[]{:T(128)}) all-reduce(f32[]{:T(128)} %get-tuple-element.25, f32[]{:T(128)} %get-tuple-element.13, f32[]{:T(128)} %get-tuple-element.12, f32[]{:T(128)} %get-tuple-element.22), channel_id=1, replica_groups=mesh['gx'=4,'gy'=2,'gz'=4] {'gy','gz'}, use_global_device_ids=true, to_apply=%region_7.8 | all-reduce | flops 4 | bytes 32 | tf_op jit(solution)/shard_map/psum | solution.py:55
  228.6 9.0 %all-reduce.1 = (f32[]{:T(128)}, f32[]{:T(128)}, f32[]{:T(128)}, f32[]{:T(128)}) all-reduce(f32[]{:T(128)} %get-tuple-element.14, f32[]{:T(128)} %get-tuple-element.15, f32[]{:T(128)} %get-tuple-element.16, f32[]{:T(128)} %get-tuple-element.17), channel_id=1, replica_groups=mesh['gx'=4,'gy'=2,'gz'=4] {'gx'}, use_global_device_ids=true, to_apply=%region_8.9 | all-reduce | flops 4 | bytes 32 | tf_op jit(solution)/shard_map/psum | solution.py:55
  240.1 2.5 %fusion.20 = f32[16,128,128]{2,0,1:T(8,128)S(1)} fusion(f32[16,128,128]{2,0,1:T(8,128)S(1)} %copy-done.2, f32[16,128,128]{2,0,1:T(8,128)} %get-tuple-element.30, f32[16,128,128]{2,0,1:T(8,128)} %get-tuple-element.26, f32[16,128,128]{2,1,0:T(8,128)S(1)} %copy-done, f32[]{:T(128)S(6)} %div.79), kind=kLoop, calls=%fused_computation.36 | loop fusion | flops 2621440 | bytes 5242884 | tf_op jit(solution)/shard_map/add | solution.py:79
  (72 shorter events, 58.9 us)
Async XLA Ops:
  1.5 19.1 %collective-permute-start = (f32[1,128,128]{2,0,1:T(1,128)S(1)}, f32[1,128,128]{2,0,1:T(1,128)S(1)}, u32[]{:S(2)}, u32[]{:S(2)}) collective-permute-start(f32[1,128,128]{2,0,1:T(1,128)S(1)} %bitcast.13), channel_id=1, source_target_pairs={{8,0},{16,8},{24,16},{9,1},{17,9},{25,17},{10,2},{18,10},{26,18},{... | collective-permute-start | bytes 196616 | tf_op jit(solution)/shard_map/ppermute | solution.py:17
  2.8 17.9 %collective-permute-start.2 = (f32[1,128,128]{2,0,1:T(1,128)S(1)}, f32[1,128,128]{2,0,1:T(1,128)S(1)}, u32[]{:S(2)}, u32[]{:S(2)}) collective-permute-start(f32[1,128,128]{2,0,1:T(1,128)S(1)} %bitcast.12), channel_id=1, source_target_pairs={{0,8},{8,16},{16,24},{1,9},{9,17},{17,25},{2,10},{10,18},{18,26},{... | collective-permute-start | bytes 196616 | tf_op jit(solution)/shard_map/ppermute | solution.py:16
  9.3 17.3 %collective-permute-start.1 = (f32[1,128,128]{2,0,1:T(1,128)S(1)}, f32[1,128,128]{2,0,1:T(1,128)S(1)}, u32[]{:S(2)}, u32[]{:S(2)}) collective-permute-start(f32[1,128,128]{2,0,1:T(1,128)S(1)} %bitcast.11), channel_id=1, source_target_pairs={{8,0},{16,8},{24,16},{9,1},{17,9},{25,17},{10,2},{18,10},{26,18},{... | collective-permute-start | bytes 196616 | tf_op jit(solution)/shard_map/ppermute | solution.py:17
  10.6 9.4 %copy-start.3 = (f32[16,128,128]{2,1,0:T(8,128)S(1)}, f32[16,128,128]{2,1,0:T(8,128)}, u32[]{:S(2)}) copy-start(f32[16,128,128]{2,1,0:T(8,128)} %param.5) | copy-start | bytes 3145732
  10.6 16.0 %collective-permute-start.3 = (f32[1,128,128]{2,0,1:T(1,128)S(1)}, f32[1,128,128]{2,0,1:T(1,128)S(1)}, u32[]{:S(2)}, u32[]{:S(2)}) collective-permute-start(f32[1,128,128]{2,0,1:T(1,128)S(1)} %bitcast.10), channel_id=1, source_target_pairs={{0,8},{8,16},{16,24},{1,9},{9,17},{17,25},{2,10},{10,18},{18,26},{... | collective-permute-start | bytes 196616 | tf_op jit(solution)/shard_map/ppermute | solution.py:16
  20.7 8.5 %collective-permute-start.4 = (f32[18,1,128]{2,0,1:T(8,128)S(1)}, f32[18,1,128]{2,0,1:T(8,128)S(1)}, u32[]{:S(2)}, u32[]{:S(2)}) collective-permute-start(f32[18,1,128]{2,0,1:T(8,128)S(1)} %get-tuple-element.47), channel_id=1, source_target_pairs={{4,0},{5,1},{6,2},{7,3},{12,8},{13,9},{14,10},{15,11},{20,16},{21,... | collective-permute-start | bytes 27656 | tf_op jit(solution)/shard_map/ppermute | solution.py:17
  22.0 7.2 %collective-permute-start.6 = (f32[18,1,128]{2,0,1:T(8,128)S(1)}, f32[18,1,128]{2,0,1:T(8,128)S(1)}, u32[]{:S(2)}, u32[]{:S(2)}) collective-permute-start(f32[18,1,128]{2,0,1:T(8,128)S(1)} %get-tuple-element.48), channel_id=1, source_target_pairs={{0,4},{1,5},{2,6},{3,7},{8,12},{9,13},{10,14},{11,15},{16,20},{17,... | collective-permute-start | bytes 27656 | tf_op jit(solution)/shard_map/ppermute | solution.py:16
  26.6 14.1 %collective-permute-start.7 = (f32[18,1,128]{2,0,1:T(8,128)S(1)}, f32[18,1,128]{2,0,1:T(8,128)S(1)}, u32[]{:S(2)}, u32[]{:S(2)}) collective-permute-start(f32[18,1,128]{2,0,1:T(8,128)S(1)} %get-tuple-element.49), channel_id=1, source_target_pairs={{0,4},{1,5},{2,6},{3,7},{8,12},{9,13},{10,14},{11,15},{16,20},{17,... | collective-permute-start | bytes 27656 | tf_op jit(solution)/shard_map/ppermute | solution.py:16
  27.9 12.8 %collective-permute-start.5 = (f32[18,1,128]{2,0,1:T(8,128)S(1)}, f32[18,1,128]{2,0,1:T(8,128)S(1)}, u32[]{:S(2)}, u32[]{:S(2)}) collective-permute-start(f32[18,1,128]{2,0,1:T(8,128)S(1)} %get-tuple-element.50), channel_id=1, source_target_pairs={{4,0},{5,1},{6,2},{7,3},{12,8},{13,9},{14,10},{15,11},{20,16},{21,... | collective-permute-start | bytes 27656 | tf_op jit(solution)/shard_map/ppermute | solution.py:17
  36.4 19.1 %collective-permute-start.8 = (f32[18,130,1]{1,0,2:T(8,128)S(1)}, f32[18,130,1]{1,0,2:T(8,128)S(1)}, u32[]{:S(2)}, u32[]{:S(2)}) collective-permute-start(f32[18,130,1]{1,0,2:T(8,128)S(1)} %copy.162), channel_id=1, source_target_pairs={{1,0},{2,1},{3,2},{5,4},{6,5},{7,6},{9,8},{10,9},{11,10},{13,12},{... | collective-permute-start | bytes 28088 | tf_op jit(solution)/shard_map/ppermute | solution.py:17
  37.7 15.6 %collective-permute-start.10 = (f32[18,130,1]{1,0,2:T(8,128)S(1)}, f32[18,130,1]{1,0,2:T(8,128)S(1)}, u32[]{:S(2)}, u32[]{:S(2)}) collective-permute-start(f32[18,130,1]{1,0,2:T(8,128)S(1)} %copy.168), channel_id=1, source_target_pairs={{0,1},{1,2},{2,3},{4,5},{5,6},{6,7},{8,9},{9,10},{10,11},{12,13},{... | collective-permute-start | bytes 28088 | tf_op jit(solution)/shard_map/ppermute | solution.py:16
  45.5 12.1 %collective-permute-start.9 = (f32[18,130,1]{1,0,2:T(8,128)S(1)}, f32[18,130,1]{1,0,2:T(8,128)S(1)}, u32[]{:S(2)}, u32[]{:S(2)}) collective-permute-start(f32[18,130,1]{1,0,2:T(8,128)S(1)} %copy.165), channel_id=1, source_target_pairs={{1,0},{2,1},{3,2},{5,4},{6,5},{7,6},{9,8},{10,9},{11,10},{13,12},{... | collective-permute-start | bytes 28088 | tf_op jit(solution)/shard_map/ppermute | solution.py:17
  49.2 10.5 %collective-permute-start.11 = (f32[18,130,1]{1,0,2:T(8,128)S(1)}, f32[18,130,1]{1,0,2:T(8,128)S(1)}, u32[]{:S(2)}, u32[]{:S(2)}) collective-permute-start(f32[18,130,1]{1,0,2:T(8,128)S(1)} %copy.171), channel_id=1, source_target_pairs={{0,1},{1,2},{2,3},{4,5},{5,6},{6,7},{8,9},{9,10},{10,11},{12,13},{... | collective-permute-start | bytes 28088 | tf_op jit(solution)/shard_map/ppermute | solution.py:16
  61.8 35.8 %copy-start = (f32[16,128,128]{2,1,0:T(8,128)S(1)}, f32[16,128,128]{2,1,0:T(8,128)}, u32[]{:S(2)}) copy-start(f32[16,128,128]{2,1,0:T(8,128)} %param.6) | copy-start | bytes 3145732
  103.6 4.4 %collective-permute-start.13 = (f32[1,128,128]{2,0,1:T(1,128)S(1)}, f32[1,128,128]{2,0,1:T(1,128)S(1)}, u32[]{:S(2)}, u32[]{:S(2)}) collective-permute-start(f32[1,128,128]{2,0,1:T(1,128)S(1)} %get-tuple-element.53), channel_id=1, source_target_pairs={{0,8},{8,16},{16,24},{1,9},{9,17},{17,25},{2,10},{10,18},{18,26},{... | collective-permute-start | bytes 196616 | tf_op jit(solution)/shard_map/ppermute | solution.py:16
  106.1 6.2 %collective-permute-start.12 = (f32[1,128,128]{2,0,1:T(1,128)S(1)}, f32[1,128,128]{2,0,1:T(1,128)S(1)}, u32[]{:S(2)}, u32[]{:S(2)}) collective-permute-start(f32[1,128,128]{2,0,1:T(1,128)S(1)} %get-tuple-element.54), channel_id=1, source_target_pairs={{8,0},{16,8},{24,16},{9,1},{17,9},{25,17},{10,2},{18,10},{26,18},{... | collective-permute-start | bytes 196616 | tf_op jit(solution)/shard_map/ppermute | solution.py:17
  112.3 5.4 %collective-permute-start.15 = (f32[18,1,128]{2,0,1:T(8,128)S(1)}, f32[18,1,128]{2,0,1:T(8,128)S(1)}, u32[]{:S(2)}, u32[]{:S(2)}) collective-permute-start(f32[18,1,128]{2,0,1:T(8,128)S(1)} %get-tuple-element.45), channel_id=1, source_target_pairs={{0,4},{1,5},{2,6},{3,7},{8,12},{9,13},{10,14},{11,15},{16,20},{17,... | collective-permute-start | bytes 27656 | tf_op jit(solution)/shard_map/ppermute | solution.py:16
  116.3 5.6 %collective-permute-start.14 = (f32[18,1,128]{2,0,1:T(8,128)S(1)}, f32[18,1,128]{2,0,1:T(8,128)S(1)}, u32[]{:S(2)}, u32[]{:S(2)}) collective-permute-start(f32[18,1,128]{2,0,1:T(8,128)S(1)} %get-tuple-element.46), channel_id=1, source_target_pairs={{4,0},{5,1},{6,2},{7,3},{12,8},{13,9},{14,10},{15,11},{20,16},{21,... | collective-permute-start | bytes 27656 | tf_op jit(solution)/shard_map/ppermute | solution.py:17
  126.7 6.7 %collective-permute-start.16 = (f32[18,130,1]{1,0,2:T(8,128)S(1)}, f32[18,130,1]{1,0,2:T(8,128)S(1)}, u32[]{:S(2)}, u32[]{:S(2)}) collective-permute-start(f32[18,130,1]{1,0,2:T(8,128)S(1)} %copy.182), channel_id=1, source_target_pairs={{1,0},{2,1},{3,2},{5,4},{6,5},{7,6},{9,8},{10,9},{11,10},{13,12},{... | collective-permute-start | bytes 28088 | tf_op jit(solution)/shard_map/ppermute | solution.py:17
  130.3 5.1 %collective-permute-start.17 = (f32[18,130,1]{1,0,2:T(8,128)S(1)}, f32[18,130,1]{1,0,2:T(8,128)S(1)}, u32[]{:S(2)}, u32[]{:S(2)}) collective-permute-start(f32[18,130,1]{1,0,2:T(8,128)S(1)} %copy.184), channel_id=1, source_target_pairs={{0,1},{1,2},{2,3},{4,5},{5,6},{6,7},{8,9},{9,10},{10,11},{12,13},{... | collective-permute-start | bytes 28088 | tf_op jit(solution)/shard_map/ppermute | solution.py:16
  173.0 18.1 %copy-start.1 = (f32[16,128,128]{2,0,1:T(8,128)}, f32[16,128,128]{2,0,1:T(8,128)S(1)}, u32[]{:S(2)}) copy-start(f32[16,128,128]{2,0,1:T(8,128)S(1)} %get-tuple-element.24) | copy-start | bytes 3145732
  173.1 5.8 %collective-permute-start.19 = (f32[1,128,128]{2,0,1:T(1,128)S(1)}, f32[1,128,128]{2,0,1:T(1,128)S(1)}, u32[]{:S(2)}, u32[]{:S(2)}) collective-permute-start(f32[1,128,128]{2,0,1:T(1,128)S(1)} %get-tuple-element.51), channel_id=1, source_target_pairs={{0,8},{8,16},{16,24},{1,9},{9,17},{17,25},{2,10},{10,18},{18,26},{... | collective-permute-start | bytes 196616 | tf_op jit(solution)/shard_map/ppermute | solution.py:16
  177.0 6.2 %collective-permute-start.18 = (f32[1,128,128]{2,0,1:T(1,128)S(1)}, f32[1,128,128]{2,0,1:T(1,128)S(1)}, u32[]{:S(2)}, u32[]{:S(2)}) collective-permute-start(f32[1,128,128]{2,0,1:T(1,128)S(1)} %get-tuple-element.52), channel_id=1, source_target_pairs={{8,0},{16,8},{24,16},{9,1},{17,9},{25,17},{10,2},{18,10},{26,18},{... | collective-permute-start | bytes 196616 | tf_op jit(solution)/shard_map/ppermute | solution.py:17
  183.2 3.7 %collective-permute-start.21 = (f32[18,1,128]{2,0,1:T(8,128)S(1)}, f32[18,1,128]{2,0,1:T(8,128)S(1)}, u32[]{:S(2)}, u32[]{:S(2)}) collective-permute-start(f32[18,1,128]{2,0,1:T(8,128)S(1)} %get-tuple-element.43), channel_id=1, source_target_pairs={{0,4},{1,5},{2,6},{3,7},{8,12},{9,13},{10,14},{11,15},{16,20},{17,... | collective-permute-start | bytes 27656 | tf_op jit(solution)/shard_map/ppermute | solution.py:16
  185.5 5.6 %collective-permute-start.20 = (f32[18,1,128]{2,0,1:T(8,128)S(1)}, f32[18,1,128]{2,0,1:T(8,128)S(1)}, u32[]{:S(2)}, u32[]{:S(2)}) collective-permute-start(f32[18,1,128]{2,0,1:T(8,128)S(1)} %get-tuple-element.44), channel_id=1, source_target_pairs={{4,0},{5,1},{6,2},{7,3},{12,8},{13,9},{14,10},{15,11},{20,16},{21,... | collective-permute-start | bytes 27656 | tf_op jit(solution)/shard_map/ppermute | solution.py:17
  195.9 7.1 %collective-permute-start.22 = (f32[18,130,1]{1,0,2:T(8,128)S(1)}, f32[18,130,1]{1,0,2:T(8,128)S(1)}, u32[]{:S(2)}, u32[]{:S(2)}) collective-permute-start(f32[18,130,1]{1,0,2:T(8,128)S(1)} %copy.189), channel_id=1, source_target_pairs={{1,0},{2,1},{3,2},{5,4},{6,5},{7,6},{9,8},{10,9},{11,10},{13,12},{... | collective-permute-start | bytes 28088 | tf_op jit(solution)/shard_map/ppermute | solution.py:17
  199.8 7.4 %copy-start.2 = (f32[16,128,128]{2,0,1:T(8,128)S(1)}, f32[16,128,128]{2,0,1:T(8,128)}, u32[]{:S(2)}) copy-start(f32[16,128,128]{2,0,1:T(8,128)} %copy-done.1) | copy-start | bytes 3145732
  199.8 5.3 %collective-permute-start.23 = (f32[18,130,1]{1,0,2:T(8,128)S(1)}, f32[18,130,1]{1,0,2:T(8,128)S(1)}, u32[]{:S(2)}, u32[]{:S(2)}) collective-permute-start(f32[18,130,1]{1,0,2:T(8,128)S(1)} %copy.191), channel_id=1, source_target_pairs={{0,1},{1,2},{2,3},{4,5},{5,6},{6,7},{8,9},{9,10},{10,11},{12,13},{... | collective-permute-start | bytes 28088 | tf_op jit(solution)/shard_map/ppermute | solution.py:16
